TPU v7x, 32 devices: a whole 2x2x4 slice. The times are simulated.
32 devices in a mesh: win: 8 (over z, y), tile: 4 (over x, core).
Axes of the slice: x: 2, y: 2, z: 4, core: 2. Of those that a mesh axis runs over, the one named last changes fastest.
Arguments:
- right_side: float32 [8, 2, 128, 1024], P('win', None, 'tile'), may hold values from -64 to 64
- error_weight: float32 [8, 2, 128, 1024], P('win', None, 'tile'), may hold values from 0.5 to 4
- coeffs: float32 [4, 8, 2, 128, 1024], P(None, 'win', None, 'tile'), may hold values from 0.1 to 0.4
- obs_block: int32 [8, 128], P('win', 'tile'), may hold values from 0 to 511
- obs_pos: int32 [8, 128, 128], P('win', 'tile'), may hold values from 0 to 127
- obs_weight: float32 [8, 128, 128], P('win', 'tile'), may hold values from 0.5 to 4
Outputs:
- solution_field: float32 [8, 2, 128, 1024], P('win', None, 'tile')
- residual: float32 [8, 2, 128, 1024], P('win', None, 'tile')
All inputs are finite; a program needn't handle non-finite values.
Results may differ from a plain program's by a relative error of at most 0.0001.
Values sent between devices are 32-bit elements; how exact they have to be, the bound alone decides.
A program may use at most 64 MiB of HBM per device.

v0:
```python
import jax
import jax.numpy as jnp
from jax import lax
from jax.sharding import PartitionSpec as P

ITERS = 3


def extended(block, sides, width):
    for axis, dim in sides:
        count = lax.axis_size(axis)
        forward = [(i, i + 1) for i in range(count - 1)]
        backward = [(target, source) for source, target in forward]
        low = lax.ppermute(
            lax.slice_in_dim(block, block.shape[dim] - width, None, axis=dim), axis, forward
        )
        high = lax.ppermute(lax.slice_in_dim(block, 0, width, axis=dim), axis, backward)
        block = jnp.concatenate([low, block, high], axis=dim)
    return block


def passed_along(x, axis, by):
    devices = lax.axis_size(axis)
    pairs = [(i, i + by) for i in range(devices) if 0 <= i + by < devices]
    return lax.ppermute(x, axis, pairs)


def forward(state, coeffs):
    padded = extended(state, (("tile", 2),), 1)
    north_south = padded[:, :, 2:, :] + padded[:, :, :-2, :]
    return (
        coeffs[0] * state
        + coeffs[1] * north_south
        + coeffs[2] * jnp.roll(state, -1, axis=3)
        + coeffs[3] * jnp.roll(state, 1, axis=3)
    )


def backward(state, coeffs):
    spread = extended(coeffs[1] * state, (("tile", 2),), 1)
    north_south = spread[:, :, 2:, :] + spread[:, :, :-2, :]
    return (
        coeffs[0] * state
        + north_south
        + jnp.roll(coeffs[2] * state, 1, axis=3)
        + jnp.roll(coeffs[3] * state, -1, axis=3)
    )


def observe(state, block_hot, cell_hot, obs_weight):
    width = cell_hot.shape[2]
    block_rows = state.reshape(-1, width)
    picked = jnp.dot(
        block_hot, block_rows, precision=lax.Precision.HIGHEST, preferred_element_type=jnp.float32
    )
    observed = jnp.einsum("bjc,bc->bj", cell_hot, picked, precision=lax.Precision.HIGHEST)
    weighted = observed * obs_weight[0]
    returned = jnp.einsum("bjc,bj->bc", cell_hot, weighted, precision=lax.Precision.HIGHEST)
    spread = jnp.dot(
        block_hot.T, returned, precision=lax.Precision.HIGHEST, preferred_element_type=jnp.float32
    )
    return spread.reshape(state.shape)


def on_device(right_side, error_weight, coeffs, obs_block, obs_pos, obs_weight):
    width = obs_pos.shape[2]
    block_total = right_side.size // width
    block_hot = (obs_block[0][:, None] == jnp.arange(block_total, dtype=jnp.int32)[None, :]).astype(
        jnp.float32
    )
    cell_hot = (obs_pos[0][:, :, None] == jnp.arange(width, dtype=jnp.int32)[None, None, :]).astype(
        jnp.float32
    )

    def hessian(state):
        propagated = forward(state, coeffs)
        before = passed_along(propagated, "win", 1)
        weighted = error_weight * (state - before)
        following = passed_along(weighted, "win", -1)
        return (
            weighted - backward(following, coeffs) + observe(state, block_hot, cell_hot, obs_weight)
        )

    def two_products(vector, image_vec):
        return lax.psum((jnp.sum(vector * vector), jnp.sum(vector * image_vec)), ("win", "tile"))

    solution_field = jnp.zeros_like(right_side)
    residual = right_side
    product_vec = hessian(residual)
    norm_now, product = two_products(residual, product_vec)
    step_length = norm_now / product
    direction = residual
    along = product_vec
    for iteration in range(ITERS):
        solution_field = solution_field + step_length * direction
        residual = residual - step_length * along
        if iteration + 1 < ITERS:
            product_vec = hessian(residual)
            norm_next, product = two_products(residual, product_vec)
            beta_ratio = norm_next / norm_now
            step_length = norm_next / (product - beta_ratio * norm_next / step_length)
            direction = residual + beta_ratio * direction
            along = product_vec + beta_ratio * along
            norm_now = norm_next
    return (solution_field, residual)


def solution(mesh):
    in_specs = (
        P("win", None, "tile", None),
        P("win", None, "tile", None),
        P(None, "win", None, "tile", None),
        P("win", "tile"),
        P("win", "tile", None),
        P("win", "tile", None),
    )
    out_specs = (P("win", None, "tile", None), P("win", None, "tile", None))
    return jax.shard_map(
        on_device, mesh=mesh, in_specs=in_specs, out_specs=out_specs, check_vma=False
    )
```

profile of v0, /device:TPU:0, one launch (start us, length us, event | category | flops | bytes accessed | tf_op | source)
XLA Modules:
  0.0 242.9 jit_solution(11518069762869927047)
XLA Ops:
  1.6 2.4 collective-permute-start.1
  4.0 1.3 collective-permute-start
  6.7 2.5 %collective-permute-done = f32[1,2,1,1024]{3,2,1,0:T(1,128)S(1)} collective-permute-done((f32[1,2,1,1024]{3,2,1,0:T(1,128)S(1)}, f32[1,2,1,1024]{3,2,1,0:T(1,128)S(1)}, u32[]{:S(2)}, u32[]{:S(2)}) %collective-permute-start) | collective-permute-done | bytes 8224 | tf_op jit(solution)/shard_map/ppermute | solution.py:17
  9.4 3.6 %collective-permute-start.2 = (f32[1,2,32,1024]{3,2,1,0:T(8,128)S(1)}, f32[1,2,32,1024]{3,2,1,0:T(8,128)S(1)}, u32[]{:S(2)}, u32[]{:S(2)}) collective-permute-start(f32[1,2,32,1024]{3,2,1,0:T(8,128)S(1)} %fusion.44), channel_id=1, source_target_pairs={{0,4},{4,8},{8,12},{12,16},{16,20},{20,24},{24,28},{1,5},{5,9},{9,... | collective-permute-start | bytes 786440 | tf_op jit(solution)/shard_map/ppermute | solution.py:25
  13.3 2.0 fusion.5
  15.3 3.0 %collective-permute-done.2 = f32[1,2,32,1024]{3,2,1,0:T(8,128)S(1)} collective-permute-done((f32[1,2,32,1024]{3,2,1,0:T(8,128)S(1)}, f32[1,2,32,1024]{3,2,1,0:T(8,128)S(1)}, u32[]{:S(2)}, u32[]{:S(2)}) %collective-permute-start.2) | collective-permute-done | bytes 262176 | tf_op jit(solution)/shard_map/ppermute | solution.py:25
  18.3 1.3 collective-permute-start.3
  19.6 1.5 fusion.4
  21.1 8.2 %collective-permute-done.3 = f32[1,2,32,1024]{3,2,1,0:T(8,128)S(1)} collective-permute-done((f32[1,2,32,1024]{3,2,1,0:T(8,128)S(1)}, f32[1,2,32,1024]{3,2,1,0:T(8,128)S(1)}, u32[]{:S(2)}, u32[]{:S(2)}) %collective-permute-start.3) | collective-permute-done | bytes 262176 | tf_op jit(solution)/shard_map/ppermute | solution.py:25
  29.4 2.3 collective-permute-start.5
  31.6 1.3 collective-permute-start.4
  35.5 42.5 %all-reduce.2 = (f32[]{:T(128)}, f32[]{:T(128)}) all-reduce(f32[]{:T(128)} %get-tuple-element.7, f32[]{:T(128)} %get-tuple-element.6), channel_id=1, replica_groups=mesh['win'=8,'tile'=4] {'win','tile'}, use_global_device_ids=true, to_apply=%region_1.2 | all-reduce | flops 2 | bytes 16 | tf_op jit(solution)/shard_map/psum | solution.py:85
  82.3 4.1 %collective-permute-done.6 = f32[1,2,1,1024]{3,2,1,0:T(1,128)S(1)} collective-permute-done((f32[1,2,1,1024]{3,2,1,0:T(1,128)S(1)}, f32[1,2,1,1024]{3,2,1,0:T(1,128)S(1)}, u32[]{:S(2)}, u32[]{:S(2)}) %collective-permute-start.6) | collective-permute-done | bytes 8224 | tf_op jit(solution)/shard_map/ppermute | solution.py:17
  86.6 2.7 %collective-permute-start.8 = (f32[1,2,32,1024]{3,2,1,0:T(8,128)S(1)}, f32[1,2,32,1024]{3,2,1,0:T(8,128)S(1)}, u32[]{:S(2)}, u32[]{:S(2)}) collective-permute-start(f32[1,2,32,1024]{3,2,1,0:T(8,128)S(1)} %fusion.33), channel_id=1, source_target_pairs={{0,4},{4,8},{8,12},{12,16},{16,20},{20,24},{24,28},{1,5},{5,9},{9,... | collective-permute-start | bytes 786440 | tf_op jit(solution)/shard_map/ppermute | solution.py:25
  89.5 2.0 fusion.3
  91.5 3.0 %collective-permute-done.8 = f32[1,2,32,1024]{3,2,1,0:T(8,128)S(1)} collective-permute-done((f32[1,2,32,1024]{3,2,1,0:T(8,128)S(1)}, f32[1,2,32,1024]{3,2,1,0:T(8,128)S(1)}, u32[]{:S(2)}, u32[]{:S(2)}) %collective-permute-start.8) | collective-permute-done | bytes 262176 | tf_op jit(solution)/shard_map/ppermute | solution.py:25
  94.6 1.3 collective-permute-start.9
  95.9 1.5 fusion.2
  97.4 8.2 %collective-permute-done.9 = f32[1,2,32,1024]{3,2,1,0:T(8,128)S(1)} collective-permute-done((f32[1,2,32,1024]{3,2,1,0:T(8,128)S(1)}, f32[1,2,32,1024]{3,2,1,0:T(8,128)S(1)}, u32[]{:S(2)}, u32[]{:S(2)}) %collective-permute-start.9) | collective-permute-done | bytes 262176 | tf_op jit(solution)/shard_map/ppermute | solution.py:25
  105.7 2.3 collective-permute-start.11
  111.7 1.8 multiply_reduce_fusion.2
  113.5 42.6 %all-reduce.1 = (f32[]{:T(128)}, f32[]{:T(128)}) all-reduce(f32[]{:T(128)} %get-tuple-element.5, f32[]{:T(128)} %get-tuple-element.4), channel_id=1, replica_groups=mesh['win'=8,'tile'=4] {'win','tile'}, use_global_device_ids=true, to_apply=%region_5.6 | all-reduce | flops 2 | bytes 16 | tf_op jit(solution)/shard_map/psum | solution.py:85
  163.7 4.1 %collective-permute-done.12 = f32[1,2,1,1024]{3,2,1,0:T(1,128)S(1)} collective-permute-done((f32[1,2,1,1024]{3,2,1,0:T(1,128)S(1)}, f32[1,2,1,1024]{3,2,1,0:T(1,128)S(1)}, u32[]{:S(2)}, u32[]{:S(2)}) %collective-permute-start.12) | collective-permute-done | bytes 8224 | tf_op jit(solution)/shard_map/ppermute | solution.py:17
  168.1 2.4 collective-permute-start.14
  170.7 2.0 fusion.1
  172.7 3.0 %collective-permute-done.14 = f32[1,2,32,1024]{3,2,1,0:T(8,128)S(1)} collective-permute-done((f32[1,2,32,1024]{3,2,1,0:T(8,128)S(1)}, f32[1,2,32,1024]{3,2,1,0:T(8,128)S(1)}, u32[]{:S(2)}, u32[]{:S(2)}) %collective-permute-start.14) | collective-permute-done | bytes 262176 | tf_op jit(solution)/shard_map/ppermute | solution.py:25
  177.0 1.5 fusion
  178.5 8.2 %collective-permute-done.15 = f32[1,2,32,1024]{3,2,1,0:T(8,128)S(1)} collective-permute-done((f32[1,2,32,1024]{3,2,1,0:T(8,128)S(1)}, f32[1,2,32,1024]{3,2,1,0:T(8,128)S(1)}, u32[]{:S(2)}, u32[]{:S(2)}) %collective-permute-start.15) | collective-permute-done | bytes 262176 | tf_op jit(solution)/shard_map/ppermute | solution.py:25
  186.8 2.3 collective-permute-start.17
  191.6 1.7 reshape.245
  193.5 1.8 multiply_reduce_fusion
  195.3 42.6 %all-reduce = (f32[]{:T(128)}, f32[]{:T(128)}) all-reduce(f32[]{:T(128)} %get-tuple-element.3, f32[]{:T(128)} %get-tuple-element.2), channel_id=1, replica_groups=mesh['win'=8,'tile'=4] {'win','tile'}, use_global_device_ids=true, to_apply=%region_9.10 | all-reduce | flops 2 | bytes 16 | tf_op jit(solution)/shard_map/psum | solution.py:85
  (80 shorter events, 20.8 us)
Async XLA Ops:
  0.6 5.9 %copy-start.1 = (f32[1,2,32,1024]{3,2,1,0:T(8,128)S(1)}, f32[1,2,32,1024]{3,2,1,0:T(8,128)}, u32[]{:S(2)}) copy-start(f32[1,2,32,1024]{3,2,1,0:T(8,128)} %param.6) | copy-start | bytes 786436
  0.6 8.6 %copy-start = (f32[4,1,2,32,1024]{4,3,2,1,0:T(8,128)S(1)}, f32[4,1,2,32,1024]{4,3,2,1,0:T(8,128)}, u32[]{:S(2)}) copy-start(f32[4,1,2,32,1024]{4,3,2,1,0:T(8,128)} %param.8) | copy-start | bytes 3145732
  1.6 5.0 %collective-permute-start.1 = (f32[1,2,1,1024]{3,2,1,0:T(1,128)S(1)}, f32[1,2,1,1024]{3,2,1,0:T(1,128)S(1)}, u32[]{:S(2)}, u32[]{:S(2)}) collective-permute-start(f32[1,2,1,1024]{3,2,1,0:T(1,128)S(1)} %get-tuple-element.51), channel_id=1, source_target_pairs={{0,1},{1,2},{2,3},{4,5},{5,6},{6,7},{8,9},{9,10},{10,11},{12,13},{... | collective-permute-start | bytes 24584 | tf_op jit(solution)/shard_map/ppermute | solution.py:14
  4.0 5.2 %collective-permute-start = (f32[1,2,1,1024]{3,2,1,0:T(1,128)S(1)}, f32[1,2,1,1024]{3,2,1,0:T(1,128)S(1)}, u32[]{:S(2)}, u32[]{:S(2)}) collective-permute-start(f32[1,2,1,1024]{3,2,1,0:T(1,128)S(1)} %get-tuple-element.50), channel_id=1, source_target_pairs={{1,0},{2,1},{3,2},{5,4},{6,5},{7,6},{9,8},{10,9},{11,10},{13,12},{... | collective-permute-start | bytes 24584 | tf_op jit(solution)/shard_map/ppermute | solution.py:17
  9.2 3.8 %copy-start.6 = (s32[1,32]{1,0:T(1,128)S(1)}, s32[1,32]{1,0:T(1,128)}, u32[]{:S(2)}) copy-start(s32[1,32]{1,0:T(1,128)} %param.9) | copy-start | bytes 388
  9.2 4.0 %copy-start.7 = (s32[1,32,128]{2,1,0:T(8,128)S(1)}, s32[1,32,128]{2,1,0:T(8,128)}, u32[]{:S(2)}) copy-start(s32[1,32,128]{2,1,0:T(8,128)} %param.10) | copy-start | bytes 49156
  9.4 8.8 %copy-start.2 = (f32[1,2,32,1024]{3,2,1,0:T(8,128)S(1)}, f32[1,2,32,1024]{3,2,1,0:T(8,128)}, u32[]{:S(2)}) copy-start(f32[1,2,32,1024]{3,2,1,0:T(8,128)} %param.7) | copy-start | bytes 786436
  9.4 8.8 %collective-permute-start.2 = (f32[1,2,32,1024]{3,2,1,0:T(8,128)S(1)}, f32[1,2,32,1024]{3,2,1,0:T(8,128)S(1)}, u32[]{:S(2)}, u32[]{:S(2)}) collective-permute-start(f32[1,2,32,1024]{3,2,1,0:T(8,128)S(1)} %fusion.44), channel_id=1, source_target_pairs={{0,4},{4,8},{8,12},{12,16},{16,20},{20,24},{24,28},{1,5},{5,9},{9,... | collective-permute-start | bytes 786440 | tf_op jit(solution)/shard_map/ppermute | solution.py:25
  13.2 6.3 %copy-start.5 = (f32[1,32,128]{2,1,0:T(8,128)S(1)}, f32[1,32,128]{2,1,0:T(8,128)}, u32[]{:S(2)}) copy-start(f32[1,32,128]{2,1,0:T(8,128)} %param.11) | copy-start | bytes 49156
  18.3 11.0 %collective-permute-start.3 = (f32[1,2,32,1024]{3,2,1,0:T(8,128)S(1)}, f32[1,2,32,1024]{3,2,1,0:T(8,128)S(1)}, u32[]{:S(2)}, u32[]{:S(2)}) collective-permute-start(f32[1,2,32,1024]{3,2,1,0:T(8,128)S(1)} %subtract_multiply_fusion.2), channel_id=1, source_target_pairs={{4,0},{8,4},{12,8},{16,12},{20,16},{24,20},{28,24},{5,1},{9,5},{13... | collective-permute-start | bytes 786440 | tf_op jit(solution)/shard_map/ppermute | solution.py:25
  29.4 4.3 %collective-permute-start.5 = (f32[1,2,1,1024]{3,2,1,0:T(1,128)S(1)}, f32[1,2,1,1024]{3,2,1,0:T(1,128)S(1)}, u32[]{:S(2)}, u32[]{:S(2)}) collective-permute-start(f32[1,2,1,1024]{3,2,1,0:T(1,128)S(1)} %get-tuple-element.45), channel_id=1, source_target_pairs={{0,1},{1,2},{2,3},{4,5},{5,6},{6,7},{8,9},{9,10},{10,11},{12,13},{... | collective-permute-start | bytes 24584 | tf_op jit(solution)/shard_map/ppermute | solution.py:14
  31.6 3.1 %collective-permute-start.4 = (f32[1,2,1,1024]{3,2,1,0:T(1,128)S(1)}, f32[1,2,1,1024]{3,2,1,0:T(1,128)S(1)}, u32[]{:S(2)}, u32[]{:S(2)}) collective-permute-start(f32[1,2,1,1024]{3,2,1,0:T(1,128)S(1)} %get-tuple-element.44), channel_id=1, source_target_pairs={{1,0},{2,1},{3,2},{5,4},{6,5},{7,6},{9,8},{10,9},{11,10},{13,12},{... | collective-permute-start | bytes 24584 | tf_op jit(solution)/shard_map/ppermute | solution.py:17
  79.5 2.7 %collective-permute-start.7 = (f32[1,2,1,1024]{3,2,1,0:T(1,128)S(1)}, f32[1,2,1,1024]{3,2,1,0:T(1,128)S(1)}, u32[]{:S(2)}, u32[]{:S(2)}) collective-permute-start(f32[1,2,1,1024]{3,2,1,0:T(1,128)S(1)} %get-tuple-element.43), channel_id=1, source_target_pairs={{0,1},{1,2},{2,3},{4,5},{5,6},{6,7},{8,9},{9,10},{10,11},{12,13},{... | collective-permute-start | bytes 24584 | tf_op jit(solution)/shard_map/ppermute | solution.py:14
  80.8 5.6 %collective-permute-start.6 = (f32[1,2,1,1024]{3,2,1,0:T(1,128)S(1)}, f32[1,2,1,1024]{3,2,1,0:T(1,128)S(1)}, u32[]{:S(2)}, u32[]{:S(2)}) collective-permute-start(f32[1,2,1,1024]{3,2,1,0:T(1,128)S(1)} %get-tuple-element.42), channel_id=1, source_target_pairs={{1,0},{2,1},{3,2},{5,4},{6,5},{7,6},{9,8},{10,9},{11,10},{13,12},{... | collective-permute-start | bytes 24584 | tf_op jit(solution)/shard_map/ppermute | solution.py:17
  86.6 7.9 %collective-permute-start.8 = (f32[1,2,32,1024]{3,2,1,0:T(8,128)S(1)}, f32[1,2,32,1024]{3,2,1,0:T(8,128)S(1)}, u32[]{:S(2)}, u32[]{:S(2)}) collective-permute-start(f32[1,2,32,1024]{3,2,1,0:T(8,128)S(1)} %fusion.33), channel_id=1, source_target_pairs={{0,4},{4,8},{8,12},{12,16},{16,20},{20,24},{24,28},{1,5},{5,9},{9,... | collective-permute-start | bytes 786440 | tf_op jit(solution)/shard_map/ppermute | solution.py:25
  94.6 11.1 %copy-start.3 = (f32[1,2,32,1024]{3,2,1,0:T(8,128)}, f32[1,2,32,1024]{3,2,1,0:T(8,128)S(1)}, u32[]{:S(2)}) copy-start(f32[1,2,32,1024]{3,2,1,0:T(8,128)S(1)} %subtract_multiply_fusion.1) | copy-start | bytes 786436
  94.6 11.0 %collective-permute-start.9 = (f32[1,2,32,1024]{3,2,1,0:T(8,128)S(1)}, f32[1,2,32,1024]{3,2,1,0:T(8,128)S(1)}, u32[]{:S(2)}, u32[]{:S(2)}) collective-permute-start(f32[1,2,32,1024]{3,2,1,0:T(8,128)S(1)} %subtract_multiply_fusion.1), channel_id=1, source_target_pairs={{4,0},{8,4},{12,8},{16,12},{20,16},{24,20},{28,24},{5,1},{9,5},{13... | collective-permute-start | bytes 786440 | tf_op jit(solution)/shard_map/ppermute | solution.py:25
  105.7 6.0 %collective-permute-start.11 = (f32[1,2,1,1024]{3,2,1,0:T(1,128)S(1)}, f32[1,2,1,1024]{3,2,1,0:T(1,128)S(1)}, u32[]{:S(2)}, u32[]{:S(2)}) collective-permute-start(f32[1,2,1,1024]{3,2,1,0:T(1,128)S(1)} %get-tuple-element.37), channel_id=1, source_target_pairs={{0,1},{1,2},{2,3},{4,5},{5,6},{6,7},{8,9},{9,10},{10,11},{12,13},{... | collective-permute-start | bytes 24584 | tf_op jit(solution)/shard_map/ppermute | solution.py:14
  108.0 3.7 %collective-permute-start.10 = (f32[1,2,1,1024]{3,2,1,0:T(1,128)S(1)}, f32[1,2,1,1024]{3,2,1,0:T(1,128)S(1)}, u32[]{:S(2)}, u32[]{:S(2)}) collective-permute-start(f32[1,2,1,1024]{3,2,1,0:T(1,128)S(1)} %get-tuple-element.36), channel_id=1, source_target_pairs={{1,0},{2,1},{3,2},{5,4},{6,5},{7,6},{9,8},{10,9},{11,10},{13,12},{... | collective-permute-start | bytes 24584 | tf_op jit(solution)/shard_map/ppermute | solution.py:17
  161.0 2.7 %collective-permute-start.13 = (f32[1,2,1,1024]{3,2,1,0:T(1,128)S(1)}, f32[1,2,1,1024]{3,2,1,0:T(1,128)S(1)}, u32[]{:S(2)}, u32[]{:S(2)}) collective-permute-start(f32[1,2,1,1024]{3,2,1,0:T(1,128)S(1)} %get-tuple-element.35), channel_id=1, source_target_pairs={{0,1},{1,2},{2,3},{4,5},{5,6},{6,7},{8,9},{9,10},{10,11},{12,13},{... | collective-permute-start | bytes 24584 | tf_op jit(solution)/shard_map/ppermute | solution.py:14
  162.3 5.6 %collective-permute-start.12 = (f32[1,2,1,1024]{3,2,1,0:T(1,128)S(1)}, f32[1,2,1,1024]{3,2,1,0:T(1,128)S(1)}, u32[]{:S(2)}, u32[]{:S(2)}) collective-permute-start(f32[1,2,1,1024]{3,2,1,0:T(1,128)S(1)} %get-tuple-element.34), channel_id=1, source_target_pairs={{1,0},{2,1},{3,2},{5,4},{6,5},{7,6},{9,8},{10,9},{11,10},{13,12},{... | collective-permute-start | bytes 24584 | tf_op jit(solution)/shard_map/ppermute | solution.py:17
  168.1 7.6 %collective-permute-start.14 = (f32[1,2,32,1024]{3,2,1,0:T(8,128)S(1)}, f32[1,2,32,1024]{3,2,1,0:T(8,128)S(1)}, u32[]{:S(2)}, u32[]{:S(2)}) collective-permute-start(f32[1,2,32,1024]{3,2,1,0:T(8,128)S(1)} %fusion.22), channel_id=1, source_target_pairs={{0,4},{4,8},{8,12},{12,16},{16,20},{20,24},{24,28},{1,5},{5,9},{9,... | collective-permute-start | bytes 786440 | tf_op jit(solution)/shard_map/ppermute | solution.py:25
  175.7 11.1 %copy-start.4 = (f32[1,2,32,1024]{3,2,1,0:T(8,128)}, f32[1,2,32,1024]{3,2,1,0:T(8,128)S(1)}, u32[]{:S(2)}) copy-start(f32[1,2,32,1024]{3,2,1,0:T(8,128)S(1)} %subtract_multiply_fusion) | copy-start | bytes 786436
  175.7 11.0 %collective-permute-start.15 = (f32[1,2,32,1024]{3,2,1,0:T(8,128)S(1)}, f32[1,2,32,1024]{3,2,1,0:T(8,128)S(1)}, u32[]{:S(2)}, u32[]{:S(2)}) collective-permute-start(f32[1,2,32,1024]{3,2,1,0:T(8,128)S(1)} %subtract_multiply_fusion), channel_id=1, source_target_pairs={{4,0},{8,4},{12,8},{16,12},{20,16},{24,20},{28,24},{5,1},{9,5},{13... | collective-permute-start | bytes 786440 | tf_op jit(solution)/shard_map/ppermute | solution.py:25
  186.8 6.7 %collective-permute-start.17 = (f32[1,2,1,1024]{3,2,1,0:T(1,128)S(1)}, f32[1,2,1,1024]{3,2,1,0:T(1,128)S(1)}, u32[]{:S(2)}, u32[]{:S(2)}) collective-permute-start(f32[1,2,1,1024]{3,2,1,0:T(1,128)S(1)} %get-tuple-element.29), channel_id=1, source_target_pairs={{0,1},{1,2},{2,3},{4,5},{5,6},{6,7},{8,9},{9,10},{10,11},{12,13},{... | collective-permute-start | bytes 24584 | tf_op jit(solution)/shard_map/ppermute | solution.py:14
  189.1 4.4 %collective-permute-start.16 = (f32[1,2,1,1024]{3,2,1,0:T(1,128)S(1)}, f32[1,2,1,1024]{3,2,1,0:T(1,128)S(1)}, u32[]{:S(2)}, u32[]{:S(2)}) collective-permute-start(f32[1,2,1,1024]{3,2,1,0:T(1,128)S(1)} %get-tuple-element.28), channel_id=1, source_target_pairs={{1,0},{2,1},{3,2},{5,4},{6,5},{7,6},{9,8},{10,9},{11,10},{13,12},{... | collective-permute-start | bytes 24584 | tf_op jit(solution)/shard_map/ppermute | solution.py:17
where the time goes:
time: 244 us; the launch traced here: 243 us
  blocking collectives  128 us (52%)
  waiting for transfers between devices  45.4 us (19%)
  starting transfers between devices  32.1 us (13%)
  matrix products  13.9 us (6%)
  between operations  11.1 us (5%)
  other arithmetic  6.38 us (3%)
  local copies, waits for them, and re-layouts  6.24 us (3%)
    psum x3, blocking collectives, two_products(): lax.psum((jnp.sum(vector * vector), jnp.sum(vector * image_vec)), ('win',...  128 us
    ppermute x6, waiting for transfers between devices, passed_along(): return lax.ppermute(x, axis, pairs)  33.6 us
    ppermute x6, starting transfers between devices, passed_along(): return lax.ppermute(x, axis, pairs)  12.5 us
    ppermute x6, waiting for transfers between devices, extended(): lax.ppermute(lax.slice_in_dim(block, 0, width, axis=dim), axis, backward)  11.9 us
    ppermute x6, starting transfers between devices, extended(): lax.ppermute(lax.slice_in_dim(block, block.shape[dim] - width, None, axis...  11.8 us
    ppermute x6, starting transfers between devices, extended(): lax.ppermute(lax.slice_in_dim(block, 0, width, axis=dim), axis, backward)  7.75 us
    dot_general x3, matrix products, observe(): jnp.einsum('bjc,bc->bj', cell_hot, picked, precision=lax.Precision.HIGHEST)  5.99 us
  transfers between devices with their start and end apart: 18, of which 10 were waited for; matrix products, arithmetic and copies ran while one was open for 8% of the time, Pallas kernels for 0%

commit v1 on v0

v1 whole, which is shorter than its diff:
```python
import functools

import jax
import jax.numpy as jnp
from jax import lax
from jax.experimental import pallas as pl
from jax.experimental.pallas import tpu as pltpu
from jax.sharding import PartitionSpec as P

ITERS = 3
EDGE = 8


def kernel(wins, tiles, rhs, err, cof, oblk, opos, owgt, x_out, r_out,
           v, y, w, wn, c, d, ob, u, ui, vn, z, eo, ei, go, gi, rt, home, part, red,
           x_sem, xs_sem, l_sem, h_send, h_recv, b_send, b_recv, g_send, g_recv,
           rt_send, rt_recv, rd_send, rd_recv, wn_send, wn_recv):
    me_w = lax.axis_index("win")
    me_t = lax.axis_index("tile")
    lev = lax.rem(me_w, 2)
    other = 1 - lev
    mate = me_w + 1 - 2 * lev
    has_next = me_w + 2 < wins
    has_prev = me_w >= 2
    has_north = me_t > 0
    has_south = me_t < tiles - 1
    rows, cols = v.shape[2], v.shape[3]
    count = wins * tiles
    me = me_w * tiles + me_t
    width = opos.shape[2]
    nblk = opos.shape[1]

    def remote(src, dst, ssem, rsem, win, tile):
        return pltpu.make_async_remote_copy(
            src_ref=src, dst_ref=dst, send_sem=ssem, recv_sem=rsem,
            device_id=(win, tile), device_id_type=pl.DeviceIdType.MESH)

    swaps = [
        remote(rhs.at[0, other], v.at[0, lev], xs_sem.at[0], x_sem.at[0], mate, me_t),
        remote(err.at[0, other], w.at[lev], xs_sem.at[1], x_sem.at[1], mate, me_t),
    ] + [
        remote(cof.at[k, 0, other], c.at[k, lev], xs_sem.at[2 + k], x_sem.at[2 + k], mate, me_t)
        for k in range(4)
    ]
    for s in swaps:
        s.start()
    locs = [
        pltpu.make_async_copy(rhs.at[0, lev], v.at[0, lev], l_sem.at[0]),
        pltpu.make_async_copy(err.at[0, lev], w.at[lev], l_sem.at[1]),
        pltpu.make_async_copy(rhs.at[0, other], home, l_sem.at[2]),
    ] + [
        pltpu.make_async_copy(cof.at[k, 0, lev], c.at[k, lev], l_sem.at[3 + k]) for k in range(4)
    ]
    for s in locs:
        s.start()

    @pl.when(jnp.logical_not(has_north))
    def _():
        for it in range(ITERS):
            ei[it, 0] = jnp.zeros(ei.shape[2:], jnp.float32)
            gi[it, 0] = jnp.zeros(gi.shape[2:], jnp.float32)

    @pl.when(jnp.logical_not(has_south))
    def _():
        for it in range(ITERS):
            ei[it, 1] = jnp.zeros(ei.shape[2:], jnp.float32)
            gi[it, 1] = jnp.zeros(gi.shape[2:], jnp.float32)

    @pl.when(jnp.logical_not(has_prev))
    def _():
        for it in range(ITERS):
            ui[it] = jnp.zeros(ui.shape[1:], jnp.float32)

    @pl.when(jnp.logical_not(has_next))
    def _():
        wn[...] = jnp.zeros(wn.shape, jnp.float32)
        for it in range(ITERS):
            vn[it] = jnp.zeros(vn.shape[1:], jnp.float32)

    cell = lax.broadcasted_iota(jnp.int32, (width, width), 0)
    ones = jnp.ones((8, width), jnp.float32)
    ob[lev, nblk:, :] = jnp.zeros((8, width), jnp.float32)

    def per_block(b, carry):
        hit = jnp.where(cell == opos[0, pl.ds(b, 1), :], owgt[0, pl.ds(b, 1), :], 0.0)
        total = lax.dot_general(ones, hit, (((1,), (1,)), ((), ())),
                                precision=lax.Precision.HIGHEST,
                                preferred_element_type=jnp.float32)
        ob[lev, pl.ds(b, 1), :] = total[0:1]
        return carry

    lax.fori_loop(0, nblk, per_block, 0)
    ob[lev, nblk:nblk + 1, 0:nblk] = oblk[...].astype(jnp.float32)
    ob_copy = remote(ob.at[lev], ob.at[lev], xs_sem.at[6], x_sem.at[6], mate, me_t)
    ob_copy.start()

    def arrived(k):
        return [
            lambda: remote(rhs.at[0, other], v.at[0, other], xs_sem.at[0], x_sem.at[0], mate, me_t),
            lambda: remote(err.at[0, other], w.at[other], xs_sem.at[1], x_sem.at[1], mate, me_t),
        ][k]()

    pieces = ((0, EDGE), (rows - EDGE, EDGE), (EDGE, rows - 2 * EDGE))

    def edge_copies(out, into, ssem, rsem, it):
        north = remote(out.at[it, 0], into.at[it, 1], ssem.at[it, 0], rsem.at[it, 1],
                       me_w, me_t - 1)
        south = remote(out.at[it, 1], into.at[it, 0], ssem.at[it, 1], rsem.at[it, 0],
                       me_w, me_t + 1)
        return north, south

    def edges_start(out, into, ssem, rsem, it):
        north, south = edge_copies(out, into, ssem, rsem, it)
        pl.when(has_north)(north.start)
        pl.when(has_south)(south.start)

    def edges_wait_recv(out, into, ssem, rsem, it):
        north, south = edge_copies(out, into, ssem, rsem, it)
        pl.when(has_north)(south.wait_recv)
        pl.when(has_south)(north.wait_recv)

    def edges_wait_send(out, into, ssem, rsem, it):
        north, south = edge_copies(out, into, ssem, rsem, it)
        pl.when(has_north)(north.wait_send)
        pl.when(has_south)(south.wait_send)

    def back_copy(it, k):
        lo, n = pieces[k]
        return remote(v.at[it, 0, pl.ds(lo, n)], vn.at[it, pl.ds(lo, n)],
                      b_send.at[0, it, k], b_recv.at[0, it, k], me_w - 2, me_t)

    def forth_copy(it, k):
        lo, n = pieces[k]
        return remote(u.at[1, pl.ds(lo, n)], ui.at[it, pl.ds(lo, n)],
                      b_send.at[1, it, k], b_recv.at[1, it, k], me_w + 2, me_t)

    def ret_copy(it):
        return remote(y.at[it, other], rt.at[it], rt_send.at[it], rt_recv.at[it], mate, me_t)

    row = lax.broadcasted_iota(jnp.int32, (rows, cols), 0)

    def above(a):
        return jnp.where(row == 0, 0.0, pltpu.roll(a, 1, 0))

    def below(a):
        return jnp.where(row == rows - 1, 0.0, pltpu.roll(a, rows - 1, 0))

    def east(a):
        return pltpu.roll(a, cols - 1, 1)

    def west(a):
        return pltpu.roll(a, 1, 1)

    last = rows - 1
    wn_copy = remote(w.at[0], wn, wn_send, wn_recv, me_w - 2, me_t)

    def product(it):
        for i in range(2):
            eo[it, 0, i:i + 1] = v[it, i, 0:1]
            eo[it, 1, i:i + 1] = v[it, i, last:last + 1]
        edges_start(eo, ei, h_send, h_recv, it)

        @pl.when(has_prev)
        def _():
            for k in range(3):
                back_copy(it, k).start()

        if it == 0:
            locs[1].wait()
            arrived(1).wait_recv()
            pl.when(has_prev)(wn_copy.start)
            for k in range(4):
                locs[3 + k].wait()
                swaps[2 + k].wait_recv()
        else:
            @pl.when(has_next)
            def _():
                for k in range(3):
                    forth_copy(it - 1, k).wait_send()

        for i in (1, 0):
            a = v[it, i]
            u[i] = (c[0, i] * a + c[1, i] * (above(a) + below(a))
                    + c[2, i] * east(a) + c[3, i] * west(a))
            if i == 1:
                pl.when(has_next)(forth_copy(it, 2).start)
        edges_wait_recv(eo, ei, h_send, h_recv, it)
        for i in (1, 0):
            u[i, 0:1] = u[i, 0:1] + c[1, i, 0:1] * ei[it, 0, i:i + 1]
            u[i, last:last + 1] = u[i, last:last + 1] + c[1, i, last:last + 1] * ei[it, 1, i:i + 1]

        @pl.when(has_next)
        def _():
            forth_copy(it, 0).start()
            forth_copy(it, 1).start()
            if it == 0:
                wn_copy.wait_recv()
            back_copy(it, 0).wait_recv()
            back_copy(it, 1).wait_recv()

        for side, at in ((0, 0), (1, last)):
            here = slice(at, at + 1)
            go[it, side, 0:1] = c[1, 0, here] * (w[1, here] * (v[it, 1, here] - u[0, here]))
            go[it, side, 1:2] = c[1, 1, here] * (wn[here] * (vn[it, here] - u[1, here]))
        edges_start(go, gi, g_send, g_recv, it)

        def adjoint(i, q):
            g = c[1, i] * q
            return (c[0, i] * q + (above(g) + below(g)) + west(c[2, i] * q) + east(c[3, i] * q))

        z[...] = w[1] * (v[it, 1] - u[0])
        y[it, 0] = d[0] * v[it, 0] - adjoint(0, z[...])
        pl.when(has_next)(back_copy(it, 2).wait_recv)
        y[it, 1] = (z[...] + d[1] * v[it, 1]) - adjoint(1, wn[...] * (vn[it] - u[1]))

        @pl.when(has_prev)
        def _():
            for k in range(3):
                forth_copy(it, k).wait_recv()

        y[it, 0] = y[it, 0] + w[0] * (v[it, 0] - ui[it])
        edges_wait_recv(go, gi, g_send, g_recv, it)
        for i in range(2):
            y[it, i, 0:1] = y[it, i, 0:1] - gi[it, 0, i:i + 1]
            y[it, i, last:last + 1] = y[it, i, last:last + 1] - gi[it, 1, i:i + 1]
        ret_copy(it).start()

    def folded(a):
        return jnp.sum(jnp.sum(a, axis=0).reshape(-1, 128), axis=0, keepdims=True)

    def lanes(pair):
        a = jnp.sum(pair[0] + pair[1], axis=0, keepdims=True)
        total = a[:, 0:128]
        for k in range(1, cols // 128):
            total = total + a[:, k * 128:(k + 1) * 128]
        return total

    def reduce_start(it, r, aw):
        part[it, 0:1] = lanes(r * r)
        part[it, 1:2] = lanes(r * aw)

        def send(o, carry):
            to = lax.rem(me + o, count)
            remote(part.at[it], red.at[it, me], rd_send.at[it], rd_recv.at[it],
                   to // tiles, lax.rem(to, tiles)).start()
            return carry

        lax.fori_loop(1, count, send, 0)
        red[it, me] = part[it]

    def reduce_end(it):
        most = red.at[it, pl.ds(0, count - 1)]
        pltpu.make_async_copy(most, most, rd_recv.at[it]).wait()
        total = jnp.sum(red[it], axis=0)
        both = jnp.sum(total, axis=1, keepdims=True)
        return both[0:1], both[1:2]

    locs[0].wait()
    arrived(0).wait_recv()

    def diagonal():
        remote(ob.at[lev], ob.at[other], xs_sem.at[6], x_sem.at[6], mate, me_t).wait_recv()
        per_row = cols // width
        base = lev * (rows * per_row)
        spot = lax.broadcasted_iota(jnp.int32, (rows, nblk), 0) * per_row + base
        for i in range(2):
            who = ob[i, nblk:nblk + 1, 0:nblk]
            sums = ob[i, 0:nblk, :]
            for k in range(per_row):
                hot = jnp.where((spot + k).astype(jnp.float32) == who, 1.0, 0.0)
                d[i, :, k * width:(k + 1) * width] = jnp.dot(
                    hot, sums, precision=lax.Precision.HIGHEST,
                    preferred_element_type=jnp.float32)

    diagonal()

    product(0)
    v[1] = y[0]
    reduce_start(0, v[0], y[0])
    product(1)
    g0, d0 = reduce_end(0)
    a0 = g0 / d0
    v[2] = y[0] - a0 * y[1]
    reduce_start(1, v[0] - a0 * y[0], v[2])
    product(2)
    g1, d1 = reduce_end(1)
    b1 = g1 / g0
    a1 = g1 / (d1 - b1 * g1 / a0)

    def second(r0, w0, n0, n1):
        r1 = r0 - a0 * w0
        w1 = w0 - a0 * n0
        s1 = w1 + b1 * w0
        r2 = r1 - a1 * s1
        w2 = w1 - a1 * (n1 + b1 * n0)
        return r1, s1, r2, w2

    _, _, r2, w2 = second(v[0], y[0], y[1], y[2])
    reduce_start(2, r2, w2)

    locs[2].wait()
    for it in range(ITERS):
        ret_copy(it).wait_recv()
    g2, d2 = reduce_end(2)
    b2 = g2 / g1
    a2 = g2 / (d2 - b2 * g2 / a1)

    def finish(level, r0, w0, n0, n1):
        r1, s1, r2, w2 = second(r0, w0, n0, n1)
        p1 = r1 + b1 * r0
        x_out[0, level] = (a0 * r0 + a1 * p1) + a2 * (r2 + b2 * p1)
        r_out[0, level] = r2 - a2 * (w2 + b2 * s1)

    finish(lev, v[0, lev], y[0, lev], y[1, lev], y[2, lev])
    finish(other, home[...], rt[0], rt[1], rt[2])

    for s in swaps:
        s.wait_send()
    ob_copy.wait_send()
    pl.when(has_prev)(wn_copy.wait_send)
    for it in range(ITERS):
        edges_wait_send(eo, ei, h_send, h_recv, it)
        edges_wait_send(go, gi, g_send, g_recv, it)
        ret_copy(it).wait_send()
        most = red.at[it, pl.ds(0, count - 1)]
        pltpu.make_async_copy(most, most, rd_send.at[it]).wait()

        @pl.when(has_prev)
        def _():
            for k in range(3):
                back_copy(it, k).wait_send()

    @pl.when(has_next)
    def _():
        for k in range(3):
            forth_copy(ITERS - 1, k).wait_send()


def on_device(wins, tiles, right_side, error_weight, coeffs, obs_block, obs_pos, obs_weight):
    _, levels, rows, cols = right_side.shape
    nblk, width = obs_pos.shape[1:]
    f32 = jnp.float32
    vm = functools.partial(pltpu.VMEM, dtype=f32)
    dma = pltpu.SemaphoreType.DMA
    anyspace = pl.BlockSpec(memory_space=pl.ANY)
    vmem = pl.BlockSpec(memory_space=pltpu.VMEM)
    scratch = [
        vm((ITERS, 2, rows, cols)),
        vm((ITERS, 2, rows, cols)),
        vm((2, rows, cols)),
        vm((rows, cols)),
        vm((4, 2, rows, cols)),
        vm((2, rows, cols)),
        vm((2, nblk + 8, width)),
        vm((2, rows, cols)),
        vm((ITERS, rows, cols)),
        vm((ITERS, rows, cols)),
        vm((rows, cols)),
        vm((ITERS, 2, 2, cols)),
        vm((ITERS, 2, 2, cols)),
        vm((ITERS, 2, 2, cols)),
        vm((ITERS, 2, 2, cols)),
        vm((ITERS, rows, cols)),
        vm((rows, cols)),
        vm((ITERS, 2, 128)),
        vm((ITERS, wins * tiles, 2, 128)),
        dma((7,)), dma((7,)), dma((7,)),
        dma((ITERS, 2)), dma((ITERS, 2)),
        dma((2, ITERS, 3)), dma((2, ITERS, 3)),
        dma((ITERS, 2)), dma((ITERS, 2)),
        dma((ITERS,)), dma((ITERS,)),
        dma((ITERS,)), dma((ITERS,)),
        dma, dma,
    ]
    out = jax.ShapeDtypeStruct(right_side.shape, f32)
    return pl.pallas_call(
        functools.partial(kernel, wins, tiles),
        out_shape=(out, out),
        in_specs=[anyspace, anyspace, anyspace, vmem, vmem, vmem],
        out_specs=(vmem, vmem),
        scratch_shapes=scratch,
        compiler_params=pltpu.CompilerParams(has_side_effects=True,
                                             vmem_limit_bytes=48 * 1024 * 1024),
    )(right_side, error_weight, coeffs, obs_block, obs_pos, obs_weight)


def solution(mesh):
    in_specs = (
        P("win", None, "tile", None),
        P("win", None, "tile", None),
        P(None, "win", None, "tile", None),
        P("win", "tile"),
        P("win", "tile", None),
        P("win", "tile", None),
    )
    out_specs = (P("win", None, "tile", None), P("win", None, "tile", None))
    return jax.shard_map(
        functools.partial(on_device, mesh.shape["win"], mesh.shape["tile"]),
        mesh=mesh, in_specs=in_specs, out_specs=out_specs, check_vma=False
    )
```

time: 244 us -> 65.1 us (0.27)
  blocking collectives: 128 us -> 0 us
  Pallas kernels: 0 us -> 57.4 us
  waiting for transfers between devices: 45.4 us -> 0 us
  starting transfers between devices: 32.1 us -> 0 us
  matrix products: 13.9 us -> 0 us
  between operations: 11.1 us -> 0.65 us
  other arithmetic: 6.38 us -> 0 us
    psum x3 -> x0, blocking collectives: 128 us -> none  [two_products(): lax.psum((jnp.sum(vector * vector), jnp.sum(vector * image_vec)), ('win',...]
    pallas_call x0 -> x1, Pallas kernels: none -> 57.4 us  [on_device(): pl.pallas_call(functools.partial(kernel, wins, tiles), out_shape=(out, ou...]
    ppermute x18 -> x0, waiting for transfers between devices: 45.4 us -> none  [the longest x6 33.6 us: passed_along(): return lax.ppermute(x, axis, pairs)]
    ppermute x18 -> x0, starting transfers between devices: 32.1 us -> none  [the longest x6 12.5 us: passed_along(): return lax.ppermute(x, axis, pairs)]
    dot_general x12 -> x0, matrix products: 13.9 us -> none  [the longest x3 5.99 us: observe(): jnp.einsum('bjc,bc->bj', cell_hot, picked, precision=lax.Precision.HIGHEST)]
    unnamed x16 -> x14, local copies, waits for them, and re-layouts: 0.04 us -> 6.61 us
    reduce_sum x3 -> x0, other arithmetic: 4.47 us -> none  [two_products(): jnp.sum(vector * image_vec)]
    slice x21 -> x0, local copies, waits for them, and re-layouts: 3.32 us -> none  [the longest x6 1.64 us: forward(): jnp.roll(state, 1, axis=3)]
  transfers between devices with their start and end apart: 18 -> 0, of which waited for: 10 -> 0; matrix products, arithmetic and copies ran while one was open for 8% -> 0% of each run, Pallas kernels for 0% -> 0%
where the time goes in v1:
time: 65.1 us; the launch traced here: 64.7 us
  Pallas kernels  57.4 us (88%)
  local copies, waits for them, and re-layouts  6.61 us (10%)
    pallas_call x1, Pallas kernels, on_device(): pl.pallas_call(functools.partial(kernel, wins, tiles), out_shape=(out, ou...  57.4 us
    unnamed x14, local copies, waits for them, and re-layouts  6.61 us

profile of v1, /device:TPU:0, one launch (start us, length us, event | category | flops | bytes accessed | tf_op | source)
XLA Modules:
  0.0 64.7 jit_solution(8689948244447320029)
XLA Ops:
  0.6 0.0 copy-start
  0.6 1.2 %copy-done = f32[4,1,2,32,1024]{4,3,2,1,0:T(8,128)S(1)} copy-done((f32[4,1,2,32,1024]{4,3,2,1,0:T(8,128)S(1)}, f32[4,1,2,32,1024]{4,3,2,1,0:T(8,128)}, u32[]{:S(2)}) %copy-start) | copy-done | bytes 1048600
  1.9 0.0 copy-start.1
  1.9 0.9 %copy-done.1 = f32[1,2,32,1024]{3,2,1,0:T(8,128)S(1)} copy-done((f32[1,2,32,1024]{3,2,1,0:T(8,128)S(1)}, f32[1,2,32,1024]{3,2,1,0:T(8,128)}, u32[]{:S(2)}) %copy-start.1) | copy-done | bytes 262168
  2.8 0.0 copy-start.2
  2.8 0.9 %copy-done.2 = f32[1,2,32,1024]{3,2,1,0:T(8,128)S(1)} copy-done((f32[1,2,32,1024]{3,2,1,0:T(8,128)S(1)}, f32[1,2,32,1024]{3,2,1,0:T(8,128)}, u32[]{:S(2)}) %copy-start.2) | copy-done | bytes 262168
  3.8 0.0 copy-start.3
  3.8 0.7 %copy-done.3 = s32[1,32,128]{2,1,0:T(8,128)S(1)} copy-done((s32[1,32,128]{2,1,0:T(8,128)S(1)}, s32[1,32,128]{2,1,0:T(8,128)}, u32[]{:S(2)}) %copy-start.3) | copy-done | bytes 16408
  4.5 0.0 copy-start.4
  4.5 0.7 %copy-done.4 = f32[1,32,128]{2,1,0:T(8,128)S(1)} copy-done((f32[1,32,128]{2,1,0:T(8,128)S(1)}, f32[1,32,128]{2,1,0:T(8,128)}, u32[]{:S(2)}) %copy-start.4) | copy-done | bytes 16408
  5.2 0.0 copy-start.5
  5.2 0.7 %copy-done.5 = s32[1,32]{1,0:T(1,128)S(1)} copy-done((s32[1,32]{1,0:T(1,128)S(1)}, s32[1,32]{1,0:T(1,128)}, u32[]{:S(2)}) %copy-start.5) | copy-done | bytes 152
  5.8 57.4 %shard_map.77 = (f32[1,2,32,1024]{3,2,1,0:T(8,128)S(1)}, f32[1,2,32,1024]{3,2,1,0:T(8,128)S(1)}) custom-call(f32[1,2,32,1024]{3,2,1,0:T(8,128)S(1)} %copy-done.1, f32[1,2,32,1024]{3,2,1,0:T(8,128)S(1)} %copy-done.2, f32[4,1,2,32,1024]{4,3,2,1,0:T(8,128)S(1)} %copy-done, s32[1,32]{1,0:T(1,128)S(1)} %copy-done.5, s32[1,32,128]{2,1,0:T(8,128)S(1)} %copy-done.3, ...), custom_call_target="tpu_custom_call" | custom-call | tf_op jit(solution)/shard_map/pallas_call | solution.py:376
  63.3 0.7 %copy.10 = f32[1,2,32,1024]{3,2,1,0:T(8,128)} copy(f32[1,2,32,1024]{3,2,1,0:T(8,128)S(1)} %get-tuple-element.4) | data formatting | bytes 524288
  64.0 0.7 %copy.11 = f32[1,2,32,1024]{3,2,1,0:T(8,128)} copy(f32[1,2,32,1024]{3,2,1,0:T(8,128)S(1)} %get-tuple-element.5) | data formatting | bytes 524288
Async XLA Ops:
  0.6 1.2 %copy-start = (f32[4,1,2,32,1024]{4,3,2,1,0:T(8,128)S(1)}, f32[4,1,2,32,1024]{4,3,2,1,0:T(8,128)}, u32[]{:S(2)}) copy-start(f32[4,1,2,32,1024]{4,3,2,1,0:T(8,128)} %cof.1) | copy-start | bytes 3145732
  1.9 0.9 %copy-start.1 = (f32[1,2,32,1024]{3,2,1,0:T(8,128)S(1)}, f32[1,2,32,1024]{3,2,1,0:T(8,128)}, u32[]{:S(2)}) copy-start(f32[1,2,32,1024]{3,2,1,0:T(8,128)} %rhs.1) | copy-start | bytes 786436
  2.8 0.9 %copy-start.2 = (f32[1,2,32,1024]{3,2,1,0:T(8,128)S(1)}, f32[1,2,32,1024]{3,2,1,0:T(8,128)}, u32[]{:S(2)}) copy-start(f32[1,2,32,1024]{3,2,1,0:T(8,128)} %err.1) | copy-start | bytes 786436
  3.8 0.7 %copy-start.3 = (s32[1,32,128]{2,1,0:T(8,128)S(1)}, s32[1,32,128]{2,1,0:T(8,128)}, u32[]{:S(2)}) copy-start(s32[1,32,128]{2,1,0:T(8,128)} %opos.1) | copy-start | bytes 49156
  4.5 0.7 %copy-start.4 = (f32[1,32,128]{2,1,0:T(8,128)S(1)}, f32[1,32,128]{2,1,0:T(8,128)}, u32[]{:S(2)}) copy-start(f32[1,32,128]{2,1,0:T(8,128)} %owgt.1) | copy-start | bytes 49156
  5.2 0.7 %copy-start.5 = (s32[1,32]{1,0:T(1,128)S(1)}, s32[1,32]{1,0:T(1,128)}, u32[]{:S(2)}) copy-start(s32[1,32]{1,0:T(1,128)} %oblk.1) | copy-start | bytes 388

commit v2 on v1

--- a/solution.py
+++ b/solution.py
@@ -11,8 +11,8 @@
 EDGE = 8
 
 
-def kernel(wins, tiles, rhs, err, cof, oblk, opos, owgt, x_out, r_out,
-           v, y, w, wn, c, d, ob, u, ui, vn, z, eo, ei, go, gi, rt, home, part, red,
+def kernel(wins, tiles, rhs, err, cof, oblk_in, opos_in, owgt_in, x_out, r_out,
+           obk, ops, owt, v, y, w, wn, c, d, ob, u, ui, vn, z, eo, ei, go, gi, rt, home, part, red,
            x_sem, xs_sem, l_sem, h_send, h_recv, b_send, b_recv, g_send, g_recv,
            rt_send, rt_recv, rd_send, rd_recv, wn_send, wn_recv):
     me_w = lax.axis_index("win")
@@ -25,6 +25,7 @@
     has_north = me_t > 0
     has_south = me_t < tiles - 1
     rows, cols = v.shape[2], v.shape[3]
+    oblk, opos, owgt = obk, ops, owt
     count = wins * tiles
     me = me_w * tiles + me_t
     width = opos.shape[2]
@@ -35,24 +36,32 @@
             src_ref=src, dst_ref=dst, send_sem=ssem, recv_sem=rsem,
             device_id=(win, tile), device_id_type=pl.DeviceIdType.MESH)
 
+    pieces = [(0, EDGE), (rows - EDGE, EDGE)] + [
+        (lo, EDGE) for lo in range(EDGE, rows - EDGE, EDGE)]
+    many = len(pieces)
+
     swaps = [
         remote(rhs.at[0, other], v.at[0, lev], xs_sem.at[0], x_sem.at[0], mate, me_t),
         remote(err.at[0, other], w.at[lev], xs_sem.at[1], x_sem.at[1], mate, me_t),
     ] + [
-        remote(cof.at[k, 0, other], c.at[k, lev], xs_sem.at[2 + k], x_sem.at[2 + k], mate, me_t)
-        for k in range(4)
+        remote(cof.at[:, 0, other, pl.ds(lo, n)], c.at[:, lev, pl.ds(lo, n)],
+               xs_sem.at[3 + k], x_sem.at[3 + k], mate, me_t)
+        for k, (lo, n) in enumerate(pieces)
     ]
     for s in swaps:
         s.start()
     locs = [
+        pltpu.make_async_copy(oblk_in, obk, l_sem.at[4]),
+        pltpu.make_async_copy(opos_in, ops, l_sem.at[5]),
+        pltpu.make_async_copy(owgt_in, owt, l_sem.at[6]),
         pltpu.make_async_copy(rhs.at[0, lev], v.at[0, lev], l_sem.at[0]),
         pltpu.make_async_copy(err.at[0, lev], w.at[lev], l_sem.at[1]),
         pltpu.make_async_copy(rhs.at[0, other], home, l_sem.at[2]),
-    ] + [
-        pltpu.make_async_copy(cof.at[k, 0, lev], c.at[k, lev], l_sem.at[3 + k]) for k in range(4)
+        pltpu.make_async_copy(cof.at[:, 0, lev], c.at[:, lev], l_sem.at[3]),
     ]
     for s in locs:
         s.start()
+    locs = locs[3:] + locs[:3]
 
     @pl.when(jnp.logical_not(has_north))
     def _():
@@ -77,6 +86,8 @@
         for it in range(ITERS):
             vn[it] = jnp.zeros(vn.shape[1:], jnp.float32)
 
+    for s in locs[4:]:
+        s.wait()
     cell = lax.broadcasted_iota(jnp.int32, (width, width), 0)
     ones = jnp.ones((8, width), jnp.float32)
     ob[lev, nblk:, :] = jnp.zeros((8, width), jnp.float32)
@@ -91,8 +102,10 @@
 
     lax.fori_loop(0, nblk, per_block, 0)
     ob[lev, nblk:nblk + 1, 0:nblk] = oblk[...].astype(jnp.float32)
-    ob_copy = remote(ob.at[lev], ob.at[lev], xs_sem.at[6], x_sem.at[6], mate, me_t)
+    ob_copy = remote(ob.at[lev], ob.at[lev], xs_sem.at[2], x_sem.at[2], mate, me_t)
     ob_copy.start()
+
+    states = (v.at[0], y.at[0], v.at[1])
 
     def arrived(k):
         return [
@@ -100,7 +113,6 @@
             lambda: remote(err.at[0, other], w.at[other], xs_sem.at[1], x_sem.at[1], mate, me_t),
         ][k]()
 
-    pieces = ((0, EDGE), (rows - EDGE, EDGE), (EDGE, rows - 2 * EDGE))
 
     def edge_copies(out, into, ssem, rsem, it):
         north = remote(out.at[it, 0], into.at[it, 1], ssem.at[it, 0], rsem.at[it, 1],
@@ -126,7 +138,7 @@
 
     def back_copy(it, k):
         lo, n = pieces[k]
-        return remote(v.at[it, 0, pl.ds(lo, n)], vn.at[it, pl.ds(lo, n)],
+        return remote(states[it].at[0, pl.ds(lo, n)], vn.at[it, pl.ds(lo, n)],
                       b_send.at[0, it, k], b_recv.at[0, it, k], me_w - 2, me_t)
 
     def forth_copy(it, k):
@@ -138,6 +150,7 @@
         return remote(y.at[it, other], rt.at[it], rt_send.at[it], rt_recv.at[it], mate, me_t)
 
     row = lax.broadcasted_iota(jnp.int32, (rows, cols), 0)
+    row8 = lax.broadcasted_iota(jnp.int32, (EDGE, cols), 0)
 
     def above(a):
         return jnp.where(row == 0, 0.0, pltpu.roll(a, 1, 0))
@@ -154,45 +167,96 @@
     last = rows - 1
     wn_copy = remote(w.at[0], wn, wn_send, wn_recv, me_w - 2, me_t)
 
-    def product(it):
+    def model_piece(it, i, k):
+        lo, n = pieces[k]
+        src = states[it]
+        a = src[i, lo:lo + n]
+        top = ei[it, 0, i:i + 1] if lo == 0 else src[i, lo - 1:lo]
+        bottom = ei[it, 1, i:i + 1] if lo + n == rows else src[i, lo + n:lo + n + 1]
+        sides = (jnp.where(row8 == 0, top, pltpu.roll(a, 1, 0))
+                 + jnp.where(row8 == n - 1, bottom, pltpu.roll(a, n - 1, 0)))
+        u[i, lo:lo + n] = (c[0, i, lo:lo + n] * a + c[1, i, lo:lo + n] * sides
+                           + c[2, i, lo:lo + n] * east(a) + c[3, i, lo:lo + n] * west(a))
+
+    def sends(it):
+        src = states[it]
         for i in range(2):
-            eo[it, 0, i:i + 1] = v[it, i, 0:1]
-            eo[it, 1, i:i + 1] = v[it, i, last:last + 1]
+            eo[it, 0, i:i + 1] = src[i, 0:1]
+            eo[it, 1, i:i + 1] = src[i, last:last + 1]
         edges_start(eo, ei, h_send, h_recv, it)
 
         @pl.when(has_prev)
         def _():
-            for k in range(3):
+            for k in range(many):
                 back_copy(it, k).start()
 
+    def product(it, beside):
+        src = states[it]
+        sends(it)
+        beside()
         if it == 0:
             locs[1].wait()
             arrived(1).wait_recv()
             pl.when(has_prev)(wn_copy.start)
-            for k in range(4):
-                locs[3 + k].wait()
+            locs[3].wait()
+            edges_wait_recv(eo, ei, h_send, h_recv, it)
+            for k in range(many):
                 swaps[2 + k].wait_recv()
+                model_piece(it, 1, k)
+                pl.when(has_next)(forth_copy(it, k).start)
+                model_piece(it, 0, k)
+                if k == 1:
+                    adjoint_edges(it)
         else:
             @pl.when(has_next)
             def _():
-                for k in range(3):
+                for k in range(many):
                     forth_copy(it - 1, k).wait_send()
 
-        for i in (1, 0):
-            a = v[it, i]
-            u[i] = (c[0, i] * a + c[1, i] * (above(a) + below(a))
-                    + c[2, i] * east(a) + c[3, i] * west(a))
-            if i == 1:
-                pl.when(has_next)(forth_copy(it, 2).start)
-        edges_wait_recv(eo, ei, h_send, h_recv, it)
-        for i in (1, 0):
-            u[i, 0:1] = u[i, 0:1] + c[1, i, 0:1] * ei[it, 0, i:i + 1]
-            u[i, last:last + 1] = u[i, last:last + 1] + c[1, i, last:last + 1] * ei[it, 1, i:i + 1]
+            for k in range(2, many):
+                model_piece(it, 1, k)
+                pl.when(has_next)(forth_copy(it, k).start)
+            edges_wait_recv(eo, ei, h_send, h_recv, it)
+            for k in range(2):
+                model_piece(it, 1, k)
+                pl.when(has_next)(forth_copy(it, k).start)
+            for k in range(2):
+                model_piece(it, 0, k)
+            adjoint_edges(it)
+            for k in range(2, many):
+                model_piece(it, 0, k)
+
+        def adjoint(i, q):
+            g = c[1, i] * q
+            return (c[0, i] * q + (above(g) + below(g)) + west(c[2, i] * q) + east(c[3, i] * q))
+
+        z[...] = w[1] * (src[1] - u[0])
+        y[it, 0] = d[0] * src[0] - adjoint(0, z[...])
 
         @pl.when(has_next)
         def _():
-            forth_copy(it, 0).start()
-            forth_copy(it, 1).start()
+            for k in range(2, many):
+                back_copy(it, k).wait_recv()
+
+        y[it, 1] = (z[...] + d[1] * src[1]) - adjoint(1, wn[...] * (vn[it] - u[1]))
+
+        edges_wait_recv(go, gi, g_send, g_recv, it)
+        for i in range(2):
+            y[it, i, 0:1] = y[it, i, 0:1] - gi[it, 0, i:i + 1]
+            y[it, i, last:last + 1] = y[it, i, last:last + 1] - gi[it, 1, i:i + 1]
+
+        @pl.when(has_prev)
+        def _():
+            for k in range(many):
+                forth_copy(it, k).wait_recv()
+
+        y[it, 0] = y[it, 0] + w[0] * (src[0] - ui[it])
+
+    def adjoint_edges(it):
+        src = states[it]
+
+        @pl.when(has_next)
+        def _():
             if it == 0:
                 wn_copy.wait_recv()
             back_copy(it, 0).wait_recv()
@@ -200,33 +264,9 @@
 
         for side, at in ((0, 0), (1, last)):
             here = slice(at, at + 1)
-            go[it, side, 0:1] = c[1, 0, here] * (w[1, here] * (v[it, 1, here] - u[0, here]))
+            go[it, side, 0:1] = c[1, 0, here] * (w[1, here] * (src[1, here] - u[0, here]))
             go[it, side, 1:2] = c[1, 1, here] * (wn[here] * (vn[it, here] - u[1, here]))
         edges_start(go, gi, g_send, g_recv, it)
-
-        def adjoint(i, q):
-            g = c[1, i] * q
-            return (c[0, i] * q + (above(g) + below(g)) + west(c[2, i] * q) + east(c[3, i] * q))
-
-        z[...] = w[1] * (v[it, 1] - u[0])
-        y[it, 0] = d[0] * v[it, 0] - adjoint(0, z[...])
-        pl.when(has_next)(back_copy(it, 2).wait_recv)
-        y[it, 1] = (z[...] + d[1] * v[it, 1]) - adjoint(1, wn[...] * (vn[it] - u[1]))
-
-        @pl.when(has_prev)
-        def _():
-            for k in range(3):
-                forth_copy(it, k).wait_recv()
-
-        y[it, 0] = y[it, 0] + w[0] * (v[it, 0] - ui[it])
-        edges_wait_recv(go, gi, g_send, g_recv, it)
-        for i in range(2):
-            y[it, i, 0:1] = y[it, i, 0:1] - gi[it, 0, i:i + 1]
-            y[it, i, last:last + 1] = y[it, i, last:last + 1] - gi[it, 1, i:i + 1]
-        ret_copy(it).start()
-
-    def folded(a):
-        return jnp.sum(jnp.sum(a, axis=0).reshape(-1, 128), axis=0, keepdims=True)
 
     def lanes(pair):
         a = jnp.sum(pair[0] + pair[1], axis=0, keepdims=True)
@@ -259,7 +299,7 @@
     arrived(0).wait_recv()
 
     def diagonal():
-        remote(ob.at[lev], ob.at[other], xs_sem.at[6], x_sem.at[6], mate, me_t).wait_recv()
+        remote(ob.at[lev], ob.at[other], xs_sem.at[2], x_sem.at[2], mate, me_t).wait_recv()
         per_row = cols // width
         base = lev * (rows * per_row)
         spot = lax.broadcasted_iota(jnp.int32, (rows, nblk), 0) * per_row + base
@@ -272,17 +312,22 @@
                     hot, sums, precision=lax.Precision.HIGHEST,
                     preferred_element_type=jnp.float32)
 
-    diagonal()
-
-    product(0)
-    v[1] = y[0]
-    reduce_start(0, v[0], y[0])
-    product(1)
+    product(0, diagonal)
+
+    def first_sums():
+        ret_copy(0).start()
+        reduce_start(0, v[0], y[0])
+
+    product(1, first_sums)
     g0, d0 = reduce_end(0)
     a0 = g0 / d0
-    v[2] = y[0] - a0 * y[1]
-    reduce_start(1, v[0] - a0 * y[0], v[2])
-    product(2)
+    v[1] = y[0] - a0 * y[1]
+
+    def second_sums():
+        ret_copy(1).start()
+        reduce_start(1, v[0] - a0 * y[0], v[1])
+
+    product(2, second_sums)
     g1, d1 = reduce_end(1)
     b1 = g1 / g0
     a1 = g1 / (d1 - b1 * g1 / a0)
@@ -297,6 +342,7 @@
 
     _, _, r2, w2 = second(v[0], y[0], y[1], y[2])
     reduce_start(2, r2, w2)
+    ret_copy(2).start()
 
     locs[2].wait()
     for it in range(ITERS):
@@ -327,12 +373,12 @@
 
         @pl.when(has_prev)
         def _():
-            for k in range(3):
+            for k in range(many):
                 back_copy(it, k).wait_send()
 
     @pl.when(has_next)
     def _():
-        for k in range(3):
+        for k in range(many):
             forth_copy(ITERS - 1, k).wait_send()
 
 
@@ -344,8 +390,12 @@
     dma = pltpu.SemaphoreType.DMA
     anyspace = pl.BlockSpec(memory_space=pl.ANY)
     vmem = pl.BlockSpec(memory_space=pltpu.VMEM)
+    many = rows // EDGE
     scratch = [
-        vm((ITERS, 2, rows, cols)),
+        pltpu.VMEM(obs_block.shape, jnp.int32),
+        pltpu.VMEM(obs_pos.shape, jnp.int32),
+        vm(obs_weight.shape),
+        vm((2, 2, rows, cols)),
         vm((ITERS, 2, rows, cols)),
         vm((2, rows, cols)),
         vm((rows, cols)),
@@ -364,9 +414,9 @@
         vm((rows, cols)),
         vm((ITERS, 2, 128)),
         vm((ITERS, wins * tiles, 2, 128)),
-        dma((7,)), dma((7,)), dma((7,)),
+        dma((3 + many,)), dma((3 + many,)), dma((7,)),
         dma((ITERS, 2)), dma((ITERS, 2)),
-        dma((2, ITERS, 3)), dma((2, ITERS, 3)),
+        dma((2, ITERS, many)), dma((2, ITERS, many)),
         dma((ITERS, 2)), dma((ITERS, 2)),
         dma((ITERS,)), dma((ITERS,)),
         dma((ITERS,)), dma((ITERS,)),
@@ -376,11 +426,11 @@
     return pl.pallas_call(
         functools.partial(kernel, wins, tiles),
         out_shape=(out, out),
-        in_specs=[anyspace, anyspace, anyspace, vmem, vmem, vmem],
+        in_specs=[anyspace] * 6,
         out_specs=(vmem, vmem),
         scratch_shapes=scratch,
         compiler_params=pltpu.CompilerParams(has_side_effects=True,
-                                             vmem_limit_bytes=48 * 1024 * 1024),
+                                             vmem_limit_bytes=60 * 1024 * 1024),
     )(right_side, error_weight, coeffs, obs_block, obs_pos, obs_weight)
 
 

time: 65.1 us -> 61 us (0.937)
  local copies, waits for them, and re-layouts: 6.61 us -> 2.42 us
    unnamed x14 -> x4, local copies, waits for them, and re-layouts: 6.61 us -> 2.42 us
where the time goes in v2:
time: 61 us; the launch traced here: 60.8 us
  Pallas kernels  57.7 us (95%)
  local copies, waits for them, and re-layouts  2.42 us (4%)
  between operations  0.65 us (1%)
    pallas_call x1, Pallas kernels, on_device(): pl.pallas_call(functools.partial(kernel, wins, tiles), out_shape=(out, ou...  57.7 us
    unnamed x4, local copies, waits for them, and re-layouts  2.42 us

profile of v2, /device:TPU:0, one launch (start us, length us, event | category | flops | bytes accessed | tf_op | source)
XLA Modules:
  0.0 60.8 jit_solution(10062422925399130061)
XLA Ops:
  0.6 57.7 %shard_map.77 = (f32[1,2,32,1024]{3,2,1,0:T(8,128)}, f32[1,2,32,1024]{3,2,1,0:T(8,128)}) custom-call(f32[1,2,32,1024]{3,2,1,0:T(8,128)} %rhs.1, f32[1,2,32,1024]{3,2,1,0:T(8,128)} %err.1, f32[4,1,2,32,1024]{4,3,2,1,0:T(8,128)} %cof.1, s32[1,32]{1,0:T(1,128)} %oblk_in.1, s32[1,32,128]{2,1,0:T(8,128)} %opos_in.1, f32[1,32,128]{2,1,0:T(8,128)} %owgt_in.1), custom_call_target="tpu_custom_call" | custom-call | tf_op jit(solution)/shard_map/pallas_call | solution.py:426
  58.4 0.0 copy-start
  58.4 1.7 %copy.10 = f32[1,2,32,1024]{3,2,1,0:T(8,128)} copy(f32[1,2,32,1024]{3,2,1,0:T(8,128)} %get-tuple-element.4) | data formatting | bytes 524288
  60.1 0.0 copy-done
  60.1 0.7 %copy.11 = f32[1,2,32,1024]{3,2,1,0:T(8,128)} copy(f32[1,2,32,1024]{3,2,1,0:T(8,128)S(1)} %copy-done) | data formatting | bytes 524288
Async XLA Ops:
  58.4 1.7 %copy-start = (f32[1,2,32,1024]{3,2,1,0:T(8,128)S(1)}, f32[1,2,32,1024]{3,2,1,0:T(8,128)}, u32[]{:S(2)}) copy-start(f32[1,2,32,1024]{3,2,1,0:T(8,128)} %get-tuple-element.5) | copy-start | bytes 786436
